TPU v7x, 32 devices: a whole 2x2x4 slice. The times are simulated.
32 devices in a mesh: row: 4 (over z), col: 8 (over y, x, core).
Axes of the slice: x: 2, y: 2, z: 4, core: 2. Of those that a mesh axis runs over, the one named last changes fastest.
Arguments:
- momentum: float32 [8192, 26624], P('row', 'col'), may hold values from -6 to 6
- gradient: bfloat16 [8192, 26624], P('row', 'col'), may hold values from -150 to 150
- q_basis: bfloat16 [26624, 512], P('col', 'row'), may hold values from -0.0390625 to 0.0390625
Outputs:
- momentum_next: float32 [8192, 26624], P('row', 'col')
- p_basis: float32 [8192, 512], P(('row', 'col'))
- q_next: float32 [26624, 512], P('col', 'row')
All inputs are finite; a program needn't handle non-finite values.
Results may differ from a plain program's by a relative error of at most 0.0065.
Values may be sent and summed in bfloat16 or wider, within the bound.
No kernel may reach another device: no remote copies, remote signals or barrier semaphores. Data moves between devices by JAX's collectives and lax.ppermute only.
A program may use at most 128 MiB of HBM per device.

v0:
```python
import jax
import jax.numpy as jnp
from jax import lax
from jax.sharding import PartitionSpec as P


def body(momentum, gradient, q_basis):
    buffer = momentum + gradient.astype(jnp.float32)
    buffer_low = buffer.astype(jnp.bfloat16)
    power_part = jnp.dot(
        buffer_low,
        lax.all_gather(q_basis, "row", axis=1, tiled=True),
        preferred_element_type=jnp.float32,
    )
    row_share = buffer.shape[0] // lax.axis_size("col")
    col_index = lax.axis_index("col")
    power = lax.psum(power_part, "col")
    local_gram = jnp.dot(power.T, power, precision=lax.Precision.HIGHEST)
    gram = lax.psum(local_gram, "row")
    lower = jnp.linalg.cholesky(gram)
    p_full = jax.scipy.linalg.solve_triangular(lower, power.T, lower=True).T
    p_low = p_full.astype(jnp.bfloat16)
    p_out = lax.dynamic_slice_in_dim(p_full, col_index * row_share, row_share, 0)
    right_part = jnp.einsum("ic,ir->cr", buffer_low, p_low, preferred_element_type=jnp.float32)
    right_cols = lax.psum_scatter(right_part, "row", scatter_dimension=1, tiled=True)
    sums = lax.psum(jnp.sum(right_cols * right_cols, axis=0), "col")
    q_next = right_cols / jnp.sqrt(sums + 1e-06)
    right_low = lax.all_gather(right_cols.astype(jnp.bfloat16), "row", axis=1, tiled=True)
    update = jnp.einsum("ir,cr->ic", p_low, right_low, preferred_element_type=jnp.float32)
    return (buffer - 0.1 * update, p_out, q_next)


def solution(mesh):
    return jax.shard_map(
        body,
        mesh=mesh,
        in_specs=(P("row", "col"), P("row", "col"), P("col", "row")),
        out_specs=(P("row", "col"), P(("row", "col"), None), P("col", "row")),
        check_vma=False,
    )
```

profile of v0, /device:TPU:0, one launch (start us, length us, event | category | flops | bytes accessed | tf_op | source)
XLA Modules:
  0.0 653.8 jit_solution(9504467316959625717)
XLA Ops:
  7.2 0.0 all-gather.3.cloned.1.call-start
  7.2 0.7 all-gather.3.cloned.1.call-update
  7.9 0.0 all-reduce.4.cloned.1.call-start
  7.9 72.0 %all-gather.3.cloned.1.call-done = bf16[3328,512]{1,0:T(8,128)(2,1)} async-done(((bf16[3328,128]{1,0:T(8,128)(2,1)}), bf16[3328,512]{1,0:T(8,128)(2,1)}) %all-gather.3.cloned.1.call-update) | async-done | bytes 3407888 | tf_op jit(solution)/shard_map/all_gather | solution.py:12
  80.0 19.4 %fusion.39 = f32[2048,512]{1,0:T(8,128)} fusion(bf16[3328,512]{1,0:T(8,128)(2,1)} %all-gather.3.cloned.1.call-done, f32[2048,3328]{1,0:T(8,128)} %param.3, bf16[2048,3328]{1,0:T(8,128)(2,1)} %param.4), kind=kOutput, calls=%fused_computation.77 | convolution fusion | flops 6999769088 | bytes 48496640 | tf_op jit(solution)/shard_map/dot_general | solution.py:10
  99.3 0.0 all-reduce.4.cloned.1.call-update
  99.4 0.0 all-reduce.6.cloned.1.call-start
  99.4 79.1 %all-reduce.4.cloned.1.call-done = f32[2048,512]{1,0:T(8,128)} async-done(((f32[2048,512]{1,0:T(8,128)}), f32[2048,512]{1,0:T(8,128)}) %all-reduce.4.cloned.1.call-update) | async-done | bytes 4194320 | tf_op jit(solution)/shard_map/psum | solution.py:17
  178.5 11.4 %fusion.42 = f32[512,512]{0,1:T(8,128)} fusion(f32[2048,512]{1,0:T(8,128)} %all-reduce.4.cloned.1.call-done), kind=kOutput, calls=%fused_computation.79 | convolution fusion | flops 6442450944 | bytes 5242880 | tf_op jit(solution)/shard_map/dot_general | solution.py:18
  189.9 0.0 all-reduce.6.cloned.1.call-update
  189.9 0.2 reduce-scatter.2.cloned.1.call-start
  190.2 51.9 %all-reduce.6.cloned.1.call-done = f32[512,512]{0,1:T(8,128)} async-done(((f32[512,512]{0,1:T(8,128)}), f32[512,512]{0,1:T(8,128)}) %all-reduce.6.cloned.1.call-update) | async-done | bytes 1048592 | tf_op jit(solution)/shard_map/psum | solution.py:19
  242.0 1.6 copy.7
  243.6 1.4 fusion.15
  245.1 11.7 %cholesky.104 = f32[128,128]{1,0:T(8,128)S(1)} custom-call(f32[128,128]{1,0:T(8,128)S(1)} %cholesky.266), custom_call_target="Cholesky" | custom-call | tf_op jit(solution)/shard_map/jit(cholesky)/cholesky | solution.py:20
  256.8 9.8 %custom-call.31 = f32[1,128,128]{1,2,0:T(8,128)S(1)} custom-call(f32[1,128,128]{2,1,0:T(8,128)S(1)} %get-tuple-element.35), custom_call_target="InvertDiagBlocksLowerTriangular" | custom-call | tf_op jit(solution)/shard_map/jit(cholesky)/cholesky | solution.py:20
  266.6 0.1 cholesky.224
  266.8 0.3 constant_dynamic-update-slice_fusion.3
  267.1 0.3 convolution_subtract_fusion.2
  267.4 11.7 %cholesky.217 = f32[128,128]{1,0:T(8,128)S(1)} custom-call(f32[128,128]{1,0:T(8,128)S(1)} %cholesky.270), custom_call_target="Cholesky" | custom-call | tf_op jit(solution)/shard_map/jit(cholesky)/cholesky | solution.py:20
  279.2 10.2 %custom-call.32 = f32[1,128,128]{1,2,0:T(8,128)S(1)} custom-call(f32[1,128,128]{2,1,0:T(8,128)S(1)} %get-tuple-element.32), custom_call_target="InvertDiagBlocksLowerTriangular" | custom-call | tf_op jit(solution)/shard_map/jit(cholesky)/cholesky | solution.py:20
  289.4 0.3 convolution_dynamic-update-slice_fusion
  289.7 0.4 convolution_subtract_fusion.3
  290.1 11.7 %cholesky.238 = f32[128,128]{1,0:T(8,128)S(1)} custom-call(f32[128,128]{1,0:T(8,128)S(1)} %cholesky.275), custom_call_target="Cholesky" | custom-call | tf_op jit(solution)/shard_map/jit(cholesky)/cholesky | solution.py:20
  301.8 0.7 compare_reduce_fusion.1
  302.5 9.8 %custom-call.33 = f32[1,128,128]{1,2,0:T(8,128)S(1)} custom-call(f32[1,128,128]{2,1,0:T(8,128)S(1)} %get-tuple-element.29), custom_call_target="InvertDiagBlocksLowerTriangular" | custom-call | tf_op jit(solution)/shard_map/jit(cholesky)/cholesky | solution.py:20
  312.3 0.2 convolution_dynamic-update-slice_fusion.1
  312.5 0.4 convolution_subtract_fusion.4
  312.9 11.7 %cholesky.255 = f32[128,128]{1,0:T(8,128)S(1)} custom-call(f32[128,128]{1,0:T(8,128)S(1)} %convolution_subtract_fusion.4), custom_call_target="Cholesky" | custom-call | tf_op jit(solution)/shard_map/jit(cholesky)/cholesky | solution.py:20
  324.6 0.7 compare_reduce_fusion
  325.3 0.7 compare_reduce_fusion.2
  328.6 0.3 select_select_fusion
  328.9 10.4 %while.1 = (s32[]{:T(128)}, f32[512,512]{1,0:T(8,128)S(1)}, s32[4,2]{0,1:T(2,128)S(1)}, f32[4,128,128]{2,1,0:T(8,128)}, s32[]{:T(128)}) while((s32[]{:T(128)}, f32[512,512]{1,0:T(8,128)S(1)}, s32[4,2]{0,1:T(2,128)S(1)}, f32[4,128,128]{2,1,0:T(8,128)}, s32[]{:T(128)}) %tuple.33), condition=%wide.while_cond, body=%wide.while_body.sunk | while | flops 2 | bytes 132205 | solution.py:21
  328.9 0.1 constant_dynamic-slice_fusion.2
  329.0 0.5 fusion.53
  329.5 2.0 bitcast_dynamic-update-slice_fusion.2
  331.5 0.1 constant_dynamic-slice_fusion.2
  331.6 0.5 fusion.53
  332.1 2.0 bitcast_dynamic-update-slice_fusion.2
  334.1 0.1 constant_dynamic-slice_fusion.2
  334.1 0.5 fusion.53
  334.7 2.0 bitcast_dynamic-update-slice_fusion.2
  336.7 0.1 constant_dynamic-slice_fusion.2
  336.7 0.5 fusion.53
  337.3 2.0 bitcast_dynamic-update-slice_fusion.2
  339.2 40.2 %custom-call.34 = f32[4,128,128]{1,2,0:T(8,128)S(1)} custom-call(f32[4,128,128]{2,1,0:T(8,128)} %get-tuple-element.10), custom_call_target="InvertDiagBlocksLowerTriangular" | custom-call | tf_op jit(solution)/shard_map/jit(_solve_triangular)/triangular_solve | solution.py:21
  379.4 2.4 fusion.13
  381.9 3.0 convolution_subtract_fusion.1
  384.9 1.1 fusion.30
  386.0 3.5 convolution_subtract_fusion
  389.6 1.1 fusion.28
  390.6 6.5 fusion.7
  397.1 2.1 fusion.27
  399.2 19.7 %fusion.17 = f32[3328,512]{1,0:T(8,128)} fusion(f32[2048,3328]{1,0:T(8,128)} %param.3, bf16[2048,3328]{1,0:T(8,128)(2,1)} %param.4, f32[128,2048]{1,0:T(8,128)} %fusion.27, f32[128,2048]{1,0:T(8,128)S(1)} %fusion.28, f32[128,2048]{1,0:T(8,128)S(1)} %fusion.30, f32[128,2048]{1,0:T(8,128)S(1)} %fusion.13), kind=kOutput, calls=%fused_computation.30 | convolution fusion | flops 7008157696 | bytes 51904512 | tf_op jit(solution)/shard_map/ic,ir->cr/dot_general | solution.py:24
  418.9 0.0 all-gather.5.cloned.1.call-start
  419.0 118.7 %reduce-scatter.2.cloned.1.call-done = f32[3328,128]{1,0:T(8,128)} async-done(((f32[3328,512]{1,0:T(8,128)}), f32[3328,128]{1,0:T(8,128)}) %reduce-scatter.2.cloned.1.call-update) | async-done | bytes 1703952 | tf_op jit(solution)/shard_map/reduce_scatter | solution.py:25
  537.6 1.9 multiply_reduce_fusion
  539.5 13.6 %psum.23 = f32[128]{0:T(128)S(1)} all-reduce(f32[128]{0:T(128)S(1)} %multiply_reduce_fusion), channel_id=1, replica_groups=mesh['row'=4,'col'=8] {'col'}, use_global_device_ids=true, to_apply=%region_12.13 | all-reduce | flops 128 | bytes 1024 | tf_op jit(solution)/shard_map/psum | solution.py:26
  553.1 3.7 broadcast_divide_fusion
  556.8 1.5 pad_maximum_fusion
  558.3 0.8 dynamic-slice_bitcast_fusion
  559.2 2.0 copy.8
  561.2 62.1 %all-gather.5.cloned.1.call-done = bf16[3328,512]{1,0:T(8,128)(2,1)} async-done(((bf16[3328,128]{1,0:T(8,128)(2,1)}), bf16[3328,512]{1,0:T(8,128)(2,1)}) %all-gather.5.cloned.1.call-update) | async-done | bytes 3407888 | tf_op jit(solution)/shard_map/all_gather | solution.py:28
  623.3 23.8 %multiply_subtract_fusion = f32[2048,3328]{1,0:T(8,128)} fusion(f32[2048,3328]{1,0:T(8,128)} %param.3, bf16[2048,3328]{1,0:T(8,128)(2,1)} %param.4, bf16[3328,512]{1,0:T(8,128)(2,1)} %all-gather.5.cloned.1.call-done, f32[128,2048]{1,0:T(8,128)} %fusion.27, f32[128,2048]{1,0:T(8,128)S(1)} %fusion.28, f32[128,2048]{1,0:T(8,128)S(1)} %fusion.30, ...), kind=kOutput, calls=%fused_computation.2 | convolution fusion | flops 7014973440 | bytes 75759616 | tf_op jit(solution)/shard_map/ir,cr->ic/dot_general | solution.py:29
  (17 shorter events, 0.2 us)
Async XLA Ops:
  7.2 72.8 %all-gather.3.cloned.1.call-start = ((), (), s32[]{:S(2)}) async-start(), calls=%async_computation.1 | async-start | bytes 4259840 | tf_op jit(solution)/shard_map/all_gather | solution.py:12
  7.9 170.6 %all-reduce.4.cloned.1.call-start = ((), (), s32[]{:S(2)}) async-start(), calls=%async_computation.2 | async-start | bytes 8388608 | tf_op jit(solution)/shard_map/psum | solution.py:17
  99.4 142.7 %all-reduce.6.cloned.1.call-start = ((), (), s32[]{:S(2)}) async-start(), calls=%async_computation.3 | async-start | bytes 2097152 | tf_op jit(solution)/shard_map/psum | solution.py:19
  189.9 347.7 %reduce-scatter.2.cloned.1.call-start = ((), (), s32[]{:S(2)}) async-start(), calls=%async_computation.4 | async-start | bytes 8519680 | tf_op jit(solution)/shard_map/reduce_scatter | solution.py:25
  339.2 46.8 %copy-start.1 = (f32[512,512]{1,0:T(8,128)}, f32[512,512]{1,0:T(8,128)S(1)}, u32[]{:S(2)}) copy-start(f32[512,512]{1,0:T(8,128)S(1)} %get-tuple-element.101) | copy-start | bytes 3145732
  379.4 6.6 %copy-start = (f32[2048,512]{1,0:T(8,128)S(1)}, f32[2048,512]{1,0:T(8,128)}, u32[]{:S(2)}) copy-start(f32[2048,512]{1,0:T(8,128)} %all-reduce.4.cloned.1.call-done) | copy-start | bytes 12582916
  418.9 204.4 %all-gather.5.cloned.1.call-start = ((), (), s32[]{:S(2)}) async-start(), calls=%async_computation.5 | async-start | bytes 4259840 | tf_op jit(solution)/shard_map/all_gather | solution.py:28
Sparse Core Ops, SparseCore 0:
  9.5 70.3 all-gather.2
  99.5 78.9 all-reduce.3
  190.1 51.9 all-reduce.5
  419.0 118.5 reduce-scatter.1
  556.9 66.3 all-gather.4
where the time goes:
time: 660 us; the launch traced here: 654 us
  waiting for transfers between devices  384 us (58%)
  other arithmetic  128 us (19%)
  matrix products  95.8 us (15%)
  between operations  16.8 us (3%)
  local copies, waits for them, and re-layouts  14.9 us (2%)
  blocking collectives  13.6 us (2%)
    reduce_scatter x1, waiting for transfers between devices, body(): lax.psum_scatter(right_part, 'row', scatter_dimension=1, tiled=True)  119 us
    psum x1, waiting for transfers between devices, body(): power = lax.psum(power_part, 'col')  79.1 us
    another operation x14, other arithmetic, body(): lower = jnp.linalg.cholesky(gram)  78.8 us
    all_gather x1, waiting for transfers between devices, body(): lax.all_gather(q_basis, 'row', axis=1, tiled=True)  72 us
    all_gather x1, waiting for transfers between devices, body(): lax.all_gather(right_cols.astype(jnp.bfloat16), 'row', axis=1, tiled=True)  62.1 us
    psum x1, waiting for transfers between devices, body(): gram = lax.psum(local_gram, 'row')  51.9 us
    another operation x4, other arithmetic, body(): p_full = jax.scipy.linalg.solve_triangular(lower, power.T, lower=True).T  42 us
    dot_general x1, matrix products, body(): jnp.einsum('ir,cr->ic', p_low, right_low, preferred_element_type=jnp.floa...  23.8 us
  transfers between devices with their start and end apart: 5, of which 5 were waited for; matrix products, arithmetic and copies ran while one was open for 1% of the time, Pallas kernels for 0%

commit v1 on v0

--- a/solution.py
+++ b/solution.py
@@ -14,7 +14,8 @@
     )
     row_share = buffer.shape[0] // lax.axis_size("col")
     col_index = lax.axis_index("col")
-    power = lax.psum(power_part, "col")
+    a_now = lax.all_gather(power_part, "col")
+    power = jnp.sum(a_now, axis=0)
     local_gram = jnp.dot(power.T, power, precision=lax.Precision.HIGHEST)
     gram = lax.psum(local_gram, "row")
     lower = jnp.linalg.cholesky(gram)

time: 660 us -> 756 us (1.15)
  waiting for transfers between devices: 384 us -> 464 us
  other arithmetic: 128 us -> 143 us
    all_gather x0 -> x1, waiting for transfers between devices: none -> 159 us  [body(): a_now = lax.all_gather(power_part, 'col')]
    psum x1 -> x0, waiting for transfers between devices: 79.1 us -> none  [body(): power = lax.psum(power_part, 'col')]
    reduce_sum x0 -> x1, other arithmetic: none -> 15.1 us  [body(): power = jnp.sum(a_now, axis=0)]
where the time goes in v1:
time: 756 us; the launch traced here: 749 us
  waiting for transfers between devices  464 us (61%)
  other arithmetic  143 us (19%)
  matrix products  96 us (13%)
  between operations  16.8 us (2%)
  local copies, waits for them, and re-layouts  15.5 us (2%)
  blocking collectives  13.5 us (2%)
    all_gather x1, waiting for transfers between devices, body(): a_now = lax.all_gather(power_part, 'col')  159 us
    reduce_scatter x1, waiting for transfers between devices, body(): lax.psum_scatter(right_part, 'row', scatter_dimension=1, tiled=True)  119 us
    another operation x14, other arithmetic, body(): lower = jnp.linalg.cholesky(gram)  78.8 us
    all_gather x1, waiting for transfers between devices, body(): lax.all_gather(q_basis, 'row', axis=1, tiled=True)  72 us
    all_gather x1, waiting for transfers between devices, body(): lax.all_gather(right_cols.astype(jnp.bfloat16), 'row', axis=1, tiled=True)  62.1 us
    psum x1, waiting for transfers between devices, body(): gram = lax.psum(local_gram, 'row')  51.8 us
    another operation x4, other arithmetic, body(): p_full = jax.scipy.linalg.solve_triangular(lower, power.T, lower=True).T  42 us
    dot_general x1, matrix products, body(): jnp.einsum('ir,cr->ic', p_low, right_low, preferred_element_type=jnp.floa...  23.8 us
  transfers between devices with their start and end apart: 5, of which 5 were waited for; matrix products, arithmetic and copies ran while one was open for 1% of the time, Pallas kernels for 0%

profile of v1, /device:TPU:0, one launch (start us, length us, event | category | flops | bytes accessed | tf_op | source)
XLA Modules:
  0.0 749.4 jit_solution(10172843686284890210)
XLA Ops:
  7.2 0.0 all-gather.5.cloned.1.call-start
  7.2 0.7 all-gather.5.cloned.1.call-update
  7.9 0.0 all-gather.9.cloned.1.call-start
  7.9 72.0 %all-gather.5.cloned.1.call-done = bf16[3328,512]{1,0:T(8,128)(2,1)} async-done(((bf16[3328,128]{1,0:T(8,128)(2,1)}), bf16[3328,512]{1,0:T(8,128)(2,1)}) %all-gather.5.cloned.1.call-update) | async-done | bytes 3407888 | tf_op jit(solution)/shard_map/all_gather | solution.py:12
  80.0 19.4 %fusion.39 = f32[2048,512]{1,0:T(8,128)} fusion(bf16[3328,512]{1,0:T(8,128)(2,1)} %all-gather.5.cloned.1.call-done, f32[2048,3328]{1,0:T(8,128)} %param.3, bf16[2048,3328]{1,0:T(8,128)(2,1)} %param.4), kind=kOutput, calls=%fused_computation.77 | convolution fusion | flops 6999769088 | bytes 48496640 | tf_op jit(solution)/shard_map/dot_general | solution.py:10
  99.3 0.0 all-gather.9.cloned.1.call-update
  99.4 0.0 all-reduce.3.cloned.1.call-start
  99.4 159.0 %all-gather.9.cloned.1.call-done = f32[16384,512]{1,0:T(8,128)} async-done(((f32[2048,512]{1,0:T(8,128)}), f32[16384,512]{1,0:T(8,128)}) %all-gather.9.cloned.1.call-update) | async-done | bytes 33554448 | tf_op jit(solution)/shard_map/all_gather | solution.py:17
  258.4 15.1 %reduce_sum.18 = f32[2048,512]{1,0:T(8,128)} reduce(f32[8,2048,512]{2,1,0:T(8,128)} %bitcast.60, f32[]{:T(128)} %constant.147.clone.1), dimensions={0}, to_apply=%region_0.0 | reduce | flops 7340032 | bytes 37748740 | tf_op jit(solution)/shard_map/reduce_sum | solution.py:18
  273.4 11.6 %fusion.42 = f32[512,512]{0,1:T(8,128)} fusion(f32[2048,512]{1,0:T(8,128)} %reduce_sum.18), kind=kOutput, calls=%fused_computation.79 | convolution fusion | flops 6442450944 | bytes 5242880 | tf_op jit(solution)/shard_map/dot_general | solution.py:19
  285.0 0.2 reduce-scatter.2.cloned.1.call-start
  285.2 51.8 %all-reduce.3.cloned.1.call-done = f32[512,512]{0,1:T(8,128)} async-done(((f32[512,512]{0,1:T(8,128)}), f32[512,512]{0,1:T(8,128)}) %all-reduce.3.cloned.1.call-update) | async-done | bytes 1048592 | tf_op jit(solution)/shard_map/psum | solution.py:20
  337.1 1.6 copy.7
  338.6 1.4 fusion.15
  340.1 11.7 %cholesky.104 = f32[128,128]{1,0:T(8,128)S(1)} custom-call(f32[128,128]{1,0:T(8,128)S(1)} %cholesky.266), custom_call_target="Cholesky" | custom-call | tf_op jit(solution)/shard_map/jit(cholesky)/cholesky | solution.py:21
  351.8 0.1 cholesky.224
  352.0 9.8 %custom-call.31 = f32[1,128,128]{1,2,0:T(8,128)S(1)} custom-call(f32[1,128,128]{2,1,0:T(8,128)S(1)} %get-tuple-element.35), custom_call_target="InvertDiagBlocksLowerTriangular" | custom-call | tf_op jit(solution)/shard_map/jit(cholesky)/cholesky | solution.py:21
  361.8 0.3 constant_dynamic-update-slice_fusion.3
  362.1 0.3 convolution_subtract_fusion.2
  362.4 11.7 %cholesky.217 = f32[128,128]{1,0:T(8,128)S(1)} custom-call(f32[128,128]{1,0:T(8,128)S(1)} %cholesky.270), custom_call_target="Cholesky" | custom-call | tf_op jit(solution)/shard_map/jit(cholesky)/cholesky | solution.py:21
  374.2 10.2 %custom-call.32 = f32[1,128,128]{1,2,0:T(8,128)S(1)} custom-call(f32[1,128,128]{2,1,0:T(8,128)S(1)} %get-tuple-element.32), custom_call_target="InvertDiagBlocksLowerTriangular" | custom-call | tf_op jit(solution)/shard_map/jit(cholesky)/cholesky | solution.py:21
  384.4 0.3 convolution_dynamic-update-slice_fusion
  384.7 0.4 convolution_subtract_fusion.3
  385.1 11.7 %cholesky.238 = f32[128,128]{1,0:T(8,128)S(1)} custom-call(f32[128,128]{1,0:T(8,128)S(1)} %cholesky.275), custom_call_target="Cholesky" | custom-call | tf_op jit(solution)/shard_map/jit(cholesky)/cholesky | solution.py:21
  396.8 0.7 compare_reduce_fusion.1
  397.5 9.8 %custom-call.33 = f32[1,128,128]{1,2,0:T(8,128)S(1)} custom-call(f32[1,128,128]{2,1,0:T(8,128)S(1)} %get-tuple-element.29), custom_call_target="InvertDiagBlocksLowerTriangular" | custom-call | tf_op jit(solution)/shard_map/jit(cholesky)/cholesky | solution.py:21
  407.3 0.2 convolution_dynamic-update-slice_fusion.1
  407.6 0.4 convolution_subtract_fusion.4
  407.9 11.7 %cholesky.255 = f32[128,128]{1,0:T(8,128)S(1)} custom-call(f32[128,128]{1,0:T(8,128)S(1)} %convolution_subtract_fusion.4), custom_call_target="Cholesky" | custom-call | tf_op jit(solution)/shard_map/jit(cholesky)/cholesky | solution.py:21
  419.7 0.6 compare_reduce_fusion
  420.3 0.7 compare_reduce_fusion.2
  423.5 0.3 select_select_fusion
  423.8 10.9 %while.1 = (s32[]{:T(128)}, f32[512,512]{1,0:T(8,128)S(1)}, s32[4,2]{0,1:T(2,128)S(1)}, f32[4,128,128]{2,1,0:T(8,128)}, s32[]{:T(128)}) while((s32[]{:T(128)}, f32[512,512]{1,0:T(8,128)S(1)}, s32[4,2]{0,1:T(2,128)S(1)}, f32[4,128,128]{2,1,0:T(8,128)}, s32[]{:T(128)}) %tuple.33), condition=%wide.while_cond, body=%wide.while_body.sunk | while | flops 2 | bytes 132705 | solution.py:22
  423.9 0.1 constant_dynamic-slice_fusion.2
  423.9 0.6 fusion.53
  424.5 2.1 bitcast_dynamic-update-slice_fusion.2
  426.6 0.1 constant_dynamic-slice_fusion.2
  426.7 0.6 fusion.53
  427.3 2.1 bitcast_dynamic-update-slice_fusion.2
  429.3 0.1 constant_dynamic-slice_fusion.2
  429.4 0.6 fusion.53
  430.0 2.1 bitcast_dynamic-update-slice_fusion.2
  432.1 0.1 constant_dynamic-slice_fusion.2
  432.1 0.6 fusion.53
  432.7 2.1 bitcast_dynamic-update-slice_fusion.2
  434.8 40.2 %custom-call.34 = f32[4,128,128]{1,2,0:T(8,128)S(1)} custom-call(f32[4,128,128]{2,1,0:T(8,128)} %get-tuple-element.10), custom_call_target="InvertDiagBlocksLowerTriangular" | custom-call | tf_op jit(solution)/shard_map/jit(_solve_triangular)/triangular_solve | solution.py:22
  475.0 2.4 fusion.13
  477.4 3.0 convolution_subtract_fusion.1
  480.5 1.1 fusion.30
  481.6 3.5 convolution_subtract_fusion
  485.1 1.1 fusion.28
  486.2 6.5 fusion.7
  492.7 2.1 fusion.27
  494.8 19.7 %fusion.17 = f32[3328,512]{1,0:T(8,128)} fusion(f32[2048,3328]{1,0:T(8,128)} %param.3, bf16[2048,3328]{1,0:T(8,128)(2,1)} %param.4, f32[128,2048]{1,0:T(8,128)} %fusion.27, f32[128,2048]{1,0:T(8,128)S(1)} %fusion.28, f32[128,2048]{1,0:T(8,128)S(1)} %fusion.30, f32[128,2048]{1,0:T(8,128)S(1)} %fusion.13), kind=kOutput, calls=%fused_computation.30 | convolution fusion | flops 7008157696 | bytes 51904512 | tf_op jit(solution)/shard_map/ic,ir->cr/dot_general | solution.py:25
  514.5 0.0 all-gather.7.cloned.1.call-start
  514.5 118.7 %reduce-scatter.2.cloned.1.call-done = f32[3328,128]{1,0:T(8,128)} async-done(((f32[3328,512]{1,0:T(8,128)}), f32[3328,128]{1,0:T(8,128)}) %reduce-scatter.2.cloned.1.call-update) | async-done | bytes 1703952 | tf_op jit(solution)/shard_map/reduce_scatter | solution.py:26
  633.2 1.9 multiply_reduce_fusion
  635.1 13.5 %psum.15 = f32[128]{0:T(128)S(1)} all-reduce(f32[128]{0:T(128)S(1)} %multiply_reduce_fusion), channel_id=1, replica_groups=mesh['row'=4,'col'=8] {'col'}, use_global_device_ids=true, to_apply=%region_12.13 | all-reduce | flops 128 | bytes 1024 | tf_op jit(solution)/shard_map/psum | solution.py:27
  648.6 3.7 broadcast_divide_fusion
  652.3 1.5 pad_maximum_fusion
  653.9 0.8 dynamic-slice_bitcast_fusion
  654.7 2.0 copy.8
  656.7 62.1 %all-gather.7.cloned.1.call-done = bf16[3328,512]{1,0:T(8,128)(2,1)} async-done(((bf16[3328,128]{1,0:T(8,128)(2,1)}), bf16[3328,512]{1,0:T(8,128)(2,1)}) %all-gather.7.cloned.1.call-update) | async-done | bytes 3407888 | tf_op jit(solution)/shard_map/all_gather | solution.py:29
  718.8 23.8 %multiply_subtract_fusion = f32[2048,3328]{1,0:T(8,128)} fusion(f32[2048,3328]{1,0:T(8,128)} %param.3, bf16[2048,3328]{1,0:T(8,128)(2,1)} %param.4, bf16[3328,512]{1,0:T(8,128)(2,1)} %all-gather.7.cloned.1.call-done, f32[128,2048]{1,0:T(8,128)} %fusion.27, f32[128,2048]{1,0:T(8,128)S(1)} %fusion.28, f32[128,2048]{1,0:T(8,128)S(1)} %fusion.30, ...), kind=kOutput, calls=%fused_computation.2 | convolution fusion | flops 7014973440 | bytes 75759616 | tf_op jit(solution)/shard_map/ir,cr->ic/dot_general | solution.py:30
  (18 shorter events, 0.2 us)
Async XLA Ops:
  7.2 72.8 %all-gather.5.cloned.1.call-start = ((), (), s32[]{:S(2)}) async-start(), calls=%async_computation.1 | async-start | bytes 4259840 | tf_op jit(solution)/shard_map/all_gather | solution.py:12
  7.9 250.5 %all-gather.9.cloned.1.call-start = ((), (), s32[]{:S(2)}) async-start(), calls=%async_computation.5 | async-start | bytes 37748736 | tf_op jit(solution)/shard_map/all_gather | solution.py:17
  99.4 237.7 %all-reduce.3.cloned.1.call-start = ((), (), s32[]{:S(2)}) async-start(), calls=%async_computation.2 | async-start | bytes 2097152 | tf_op jit(solution)/shard_map/psum | solution.py:20
  285.0 348.2 %reduce-scatter.2.cloned.1.call-start = ((), (), s32[]{:S(2)}) async-start(), calls=%async_computation.3 | async-start | bytes 8519680 | tf_op jit(solution)/shard_map/reduce_scatter | solution.py:26
  434.8 46.8 %copy-start.1 = (f32[512,512]{1,0:T(8,128)}, f32[512,512]{1,0:T(8,128)S(1)}, u32[]{:S(2)}) copy-start(f32[512,512]{1,0:T(8,128)S(1)} %get-tuple-element.101) | copy-start | bytes 3145732
  475.0 6.6 copy-start
  514.5 204.4 %all-gather.7.cloned.1.call-start = ((), (), s32[]{:S(2)}) async-start(), calls=%async_computation.4 | async-start | bytes 4259840 | tf_op jit(solution)/shard_map/all_gather | solution.py:29
Sparse Core Ops, SparseCore 0:
  9.5 70.3 all-gather.4
  99.5 158.8 all-gather.8
  285.1 51.8 all-reduce.2
  514.6 118.5 reduce-scatter.1
  652.4 66.3 all-gather.6
